TPU v7x, 32 devices: a whole 2x2x4 slice. The times are simulated.
32 devices in a mesh: row: 4 (over y, x), col: 8 (over z, core).
Axes of the slice: x: 2, y: 2, z: 4, core: 2. Of those that a mesh axis runs over, the one named last changes fastest.
Arguments:
- iterates: float32 [11, 1024], P(None, ('col', 'row')), may hold values from -6 to 6
- residuals: float32 [11, 1024], P(None, ('col', 'row')), may hold values from -3 to 3
- operator: float32 [16384, 1024], P('row', 'col'), may hold values from -0.1875 to 0.1875
- target: float32 [16384], replicated, may hold values from -6 to 6
- cone_id: int32 [16384], replicated, may hold values from 0 to 2047, never falling along the last dimension, each value on 1 to 16 neighbouring positions
Outputs:
- next_point: float32 [1024], P(('col', 'row'))
- projected: float32 [16384], P('row')
Inputs may be any that keep to these rules, and one draw needn't show every extreme that they name: cone_id never falls along the rows; each of the 2048 cones holds 1 to 16 consecutive rows.
All inputs are finite; a program needn't handle non-finite values.
Results may differ from a plain program's by a relative error of at most 0.0003.
Values sent between devices are 32-bit elements; how exact they have to be, the bound alone decides.
No kernel may reach another device: no remote copies, remote signals or barrier semaphores. Data moves between devices by JAX's collectives and lax.ppermute only.
A program may use at most 64 MiB of HBM per device.

v0:
```python
import math
import jax
import jax.numpy as jnp
from jax import lax
from jax.sharding import PartitionSpec as P

HIGH = lax.Precision.HIGHEST
RIM = 16


def with_halo(x, sides, width):
    for axis, dim in sides:
        devices, length = (lax.axis_size(axis), x.shape[dim])
        up = [(i, (i + 1) % devices) for i in range(devices - 1)]
        down = [(j, i) for i, j in up]
        last = lax.slice_in_dim(x, length - width, length, axis=dim)
        leading = lax.slice_in_dim(x, 0, width, axis=dim)
        before = lax.ppermute(last, axis, up)
        after = lax.ppermute(leading, axis, down)
        x = jnp.concatenate([before, x, after], axis=dim)
    return x


def solve_weights(gram, right_side):
    count = gram.shape[0]
    shifted = gram + 0.01 * (jnp.trace(gram) / count) * jnp.eye(count, dtype=jnp.float32)
    factor = jnp.linalg.cholesky(shifted)
    return jax.scipy.linalg.cho_solve((factor, True), right_side)


def window_cones(slack_ext, ids_ext, head_ext, length):
    shifts = range(1 - RIM, RIM)
    slack_win = jnp.stack([slack_ext[RIM + s : RIM + s + length] for s in shifts])
    ids_win = jnp.stack([ids_ext[RIM + s : RIM + s + length] for s in shifts])
    head_win = jnp.stack([head_ext[RIM + s : RIM + s + length] for s in shifts])
    own_ids = ids_ext[RIM : RIM + length]
    slack = slack_ext[RIM : RIM + length]
    head_own = head_ext[RIM : RIM + length]
    same = (ids_win == own_ids[None, :]).astype(jnp.float32)
    head_row = jnp.sum(same * head_win * slack_win, axis=0)
    tail_tot = jnp.sum(same * (1.0 - head_win) * slack_win * slack_win, axis=0)
    norm_row = jnp.sqrt(tail_tot)
    inside = norm_row <= head_row
    killed = norm_row <= -head_row
    safe_norm = jnp.where(norm_row > 0, norm_row, 1.0)
    middle = 0.5 * (head_row + norm_row)
    outside = jnp.where(head_own > 0, middle, middle * slack / safe_norm)
    return jnp.where(inside, slack, jnp.where(killed, 0.0, outside))


def body(iterates, residuals, operator, target, cone_id):
    row_count = lax.axis_size("row")
    col_count = lax.axis_size("col")
    row_block = operator.shape[0]
    local_len = iterates.shape[1]
    all_rows = row_block * row_count
    scale_back = math.sqrt(local_len * row_count * col_count / all_rows)
    row_index = lax.axis_index("row")
    row_offset = row_index * row_block
    delta_x = iterates[1:] - iterates[:-1]
    delta_f = residuals[1:] - residuals[:-1]
    last_f = residuals[-1]
    gram_local = jnp.dot(delta_f, delta_f.T, precision=HIGH)
    side_local = jnp.dot(delta_f, last_f, precision=HIGH)
    anchor = iterates[-1] + last_f
    step_dirs = delta_x + delta_f
    gram, right_side = lax.psum((gram_local, side_local), ("row", "col"))
    weights = solve_weights(gram, right_side)
    blended = anchor - jnp.dot(weights, step_dirs, precision=HIGH)
    columns = operator
    partial_value = jnp.zeros((row_block,), jnp.float32) + jnp.dot(
        columns, lax.all_gather(blended, "row", axis=0, tiled=True), precision=HIGH
    )
    image_own = lax.psum(partial_value, "col")
    head_all = jnp.concatenate(
        [jnp.ones((1,), jnp.float32), (cone_id[1:] != cone_id[:-1]).astype(jnp.float32)]
    )
    ids_pad = jnp.concatenate(
        [jnp.full((RIM,), -1, jnp.int32), cone_id, jnp.full((RIM,), -1, jnp.int32)]
    )
    head_pad = jnp.concatenate(
        [jnp.zeros((RIM,), jnp.float32), head_all, jnp.zeros((RIM,), jnp.float32)]
    )
    ids_ext = lax.dynamic_slice_in_dim(ids_pad, row_offset, row_block + 2 * RIM, 0)
    head_ext = lax.dynamic_slice_in_dim(head_pad, row_offset, row_block + 2 * RIM, 0)
    slack_own = lax.dynamic_slice_in_dim(target, row_offset, row_block, 0) - image_own
    slack_ext = with_halo(slack_own, (("row", 0),), RIM)
    slack_own = slack_ext[RIM : RIM + row_block]
    proj_own = window_cones(slack_ext, ids_ext, head_ext, row_block)
    correction = proj_own - slack_own
    columns = operator
    back = lax.psum_scatter(
        jnp.dot(correction, columns, precision=HIGH), "row", scatter_dimension=0, tiled=True
    )
    next_point = blended - scale_back * back
    return (next_point, proj_own)


def solution(mesh):
    return jax.shard_map(
        body,
        mesh=mesh,
        in_specs=(P(None, ("col", "row")), P(None, ("col", "row")), P("row", "col"), P(), P()),
        out_specs=(P(("col", "row")), P("row")),
        check_vma=False,
    )
```

profile of v0, /device:TPU:0, one launch (start us, length us, event | category | flops | bytes accessed | tf_op | source)
XLA Modules:
  0.0 124.1 jit_solution(8513609570144858646)
XLA Ops:
  0.6 0.0 copy-start
  0.7 1.0 convolution_bitcast_fusion.3
  1.7 1.0 fusion.48
  2.7 42.1 %all-reduce.2 = (f32[10,10]{0,1:T(8,128)S(1)}, f32[10]{0:T(128)S(1)}) all-reduce(f32[10,10]{0,1:T(8,128)S(1)} %fusion.48, f32[10]{0:T(128)S(1)} %convolution_bitcast_fusion.3), channel_id=1, replica_groups=mesh['row'=4,'col'=8] {'row','col'}, use_global_device_ids=true, to_apply=%region_0.0 | all-reduce | flops 110 | bytes 880 | tf_op jit(solution)/shard_map/psum | solution.py:67
  44.7 0.6 select_reduce_fusion.1
  46.0 0.1 copy.20
  46.1 0.9 cholesky.17
  47.0 0.1 copy.21
  47.1 0.1 select_reduce_fusion
  47.2 0.6 compare_reduce_fusion
  47.9 0.6 select_select_fusion
  48.5 0.1 copy.23
  48.6 0.8 custom-call.10
  49.4 0.1 convolution_bitcast_fusion.2
  49.5 0.1 convolution_bitcast_fusion.1
  49.7 1.4 %fusion.56 = (u32[1]{0:T(128)}, u32[1]{0:T(128)}) fusion(u32[32]{0:T(128)} %constant.89, u32[]{:T(128)S(6)} %add.52, u32[]{:T(128)S(6)} %add.49), kind=kLoop, calls=%fused_computation.136 | loop fusion | bytes 24
  51.7 0.9 fusion
  52.6 0.2 dynamic-update-slice.3
  52.9 0.3 copy-done.2
  53.1 9.7 %all-reduce = f32[128]{0:T(128)S(1)} all-reduce(f32[128]{0:T(128)S(1)} %dynamic-update-slice.3), channel_id=1, replica_groups=mesh['row'=4,'col'=8] {'row'}, use_global_device_ids=true, to_apply=%add | all-reduce | flops 128 | bytes 1024
  62.9 0.0 copy-done
  62.9 1.8 %fusion.43 = f32[1,4096]{1,0:T(1,128)S(1)} fusion(f32[4096,128]{1,0:T(8,128)S(1)} %copy-done, f32[128]{0:T(128)S(1)} %all-reduce), kind=kOutput, calls=%fused_computation.123 | convolution fusion | flops 6291456 | bytes 2114048 | tf_op jit(solution)/shard_map/dot_general | solution.py:71
  64.7 25.9 %psum.23 = f32[4096]{0:T(1024)S(1)} all-reduce(f32[4096]{0:T(1024)S(1)} %bitcast.210), channel_id=1, replica_groups=mesh['row'=4,'col'=8] {'col'}, use_global_device_ids=true, to_apply=%region_5.6 | all-reduce | flops 4096 | bytes 32768 | tf_op jit(solution)/shard_map/psum | solution.py:74
  90.6 0.7 dynamic-slice_subtract_fusion
  91.3 0.6 fusion.55
  91.9 1.3 %collective-permute-start.1 = (f32[16]{0:T(128)}, f32[16]{0:T(128)}, u32[]{:S(2)}, u32[]{:S(2)}) collective-permute-start(f32[16]{0:T(128)} %get-tuple-element.100), channel_id=1, source_target_pairs={{8,0},{16,8},{24,16},{9,1},{17,9},{25,17},{10,2},{18,10},{26,18},{... | collective-permute-start | bytes 200 | tf_op jit(solution)/shard_map/ppermute | solution.py:19
  93.2 5.1 %collective-permute-start = (f32[16]{0:T(128)}, f32[16]{0:T(128)}, u32[]{:S(2)}, u32[]{:S(2)}) collective-permute-start(f32[16]{0:T(128)} %get-tuple-element.101), channel_id=1, source_target_pairs={{0,8},{8,16},{16,24},{1,9},{9,17},{17,25},{2,10},{10,18},{18,26},{... | collective-permute-start | bytes 200 | tf_op jit(solution)/shard_map/ppermute | solution.py:18
  98.3 0.1 fusion.2
  98.4 0.1 concatenate.41
  98.5 0.1 concatenate.42
  98.6 0.8 fusion.54
  99.4 0.2 fusion.52
  99.6 0.3 fusion.51
  99.9 0.3 fusion.53
  100.8 0.8 stack.351
  101.5 1.6 %stack.319 = s32[31,4096]{1,0:T(8,128)S(1)} concatenate(s32[1,4096]{1,0:T(1,128)} %bitcast.224, s32[1,4096]{1,0:T(1,128)} %bitcast.223, s32[1,4096]{1,0:T(1,128)} %bitcast.222, s32[1,4096]{1,0:T(1,128)} %bitcast.221, s32[1,4096]{1,0:T(1,128)} %bitcast.220, s32[1,4096]{1,0:T(1,128)} %bitcast.219, s32[1,4096]{1,0:T(1,128)} %bitcast.218, s32[1,4096]{1,0:T(1,128)} %bitcast.217, ...), dimensions={0} | concatenate | bytes 1015808 | tf_op jit(solution)/shard_map/stack | solution.py:34
  103.1 0.0 collective-permute-done.1
  103.1 1.1 pad_maximum_fusion
  104.2 1.0 fusion.3
  105.2 0.0 collective-permute-done
  105.2 1.0 fusion.17
  106.2 1.7 %pad_maximum_fusion.1 = (f32[4096]{0:T(1024)S(1)}, f32[4096]{0:T(1024)}, f32[4096]{0:T(1024)}, f32[4096]{0:T(1024)}, f32[4096]{0:T(1024)}, /*index=5*/f32[4096]{...) fusion(f32[4096]{0:T(1024)S(1)} %dynamic-slice_subtract_fusion, f32[16]{0:T(128)} %collective-permute-done), kind=kLoop, calls=%fused_computation.102 | loop fusion | flops 36864 | bytes 163904 | tf_op jit(solution)/shard_map/concatenate | solution.py:20
  108.0 4.1 %stack.383 = f32[31,4096]{1,0:T(8,128)} concatenate(f32[1,4096]{1,0:T(1,128)} %bitcast.202, f32[1,4096]{1,0:T(1,128)} %bitcast.203, f32[1,4096]{1,0:T(1,128)} %bitcast.204, f32[1,4096]{1,0:T(1,128)} %bitcast.205, f32[1,4096]{1,0:T(1,128)} %bitcast.206, f32[1,4096]{1,0:T(1,128)} %bitcast.207, f32[1,4096]{1,0:T(1,128)} %bitcast.208, f32[1,4096]{1,0:T(1,128)} %bitcast.209, ...), dimensions={0} | concatenate | bytes 1015808 | tf_op jit(solution)/shard_map/stack | solution.py:33
  112.1 1.3 %fusion.1 = (f32[4096]{0:T(1024)S(1)}, f32[4096]{0:T(1024)S(1)}) fusion(f32[31,4096]{1,0:T(8,128)} %stack.383, f32[31,4096]{1,0:T(8,128)S(1)} %stack.351, s32[31,4096]{1,0:T(8,128)S(1)} %stack.319, s32[4096]{0:T(1024)S(1)} %get-tuple-element.54), kind=kLoop, calls=%fused_computation.7 | loop fusion | flops 1134592 | bytes 1572864 | tf_op jit(solution)/shard_map/reduce_sum | solution.py:41
  113.4 0.6 fusion.49
  114.0 1.1 convolution_bitcast_fusion.4
  115.1 8.4 %all-reduce.1 = f32[128]{0:T(128)S(1)} all-reduce(f32[128]{0:T(128)S(1)} %convolution_bitcast_fusion.4), channel_id=2, replica_groups=mesh['row'=4,'col'=8] {'row'}, use_global_device_ids=true, to_apply=%region_8.9.clone | all-reduce | flops 128 | bytes 1024
  123.5 0.6 fusion.42
  (10 shorter events, 0.0 us)
Async XLA Ops:
  0.6 62.2 %copy-start = (f32[4096,128]{1,0:T(8,128)S(1)}, f32[4096,128]{1,0:T(8,128)}, u32[]{:S(2)}) copy-start(f32[4096,128]{1,0:T(8,128)} %param.7) | copy-start | bytes 6291460
  0.6 97.7 %copy-start.1 = (s32[16384]{0:T(1024)S(1)}, s32[16384]{0:T(1024)}, u32[]{:S(2)}) copy-start(s32[16384]{0:T(1024)} %param.9) | copy-start | bytes 196612
  52.6 0.5 copy-start.2
  91.9 11.2 %collective-permute-start.1 = (f32[16]{0:T(128)}, f32[16]{0:T(128)}, u32[]{:S(2)}, u32[]{:S(2)}) collective-permute-start(f32[16]{0:T(128)} %get-tuple-element.100), channel_id=1, source_target_pairs={{8,0},{16,8},{24,16},{9,1},{17,9},{25,17},{10,2},{18,10},{26,18},{... | collective-permute-start | bytes 200 | tf_op jit(solution)/shard_map/ppermute | solution.py:19
  93.2 12.0 %collective-permute-start = (f32[16]{0:T(128)}, f32[16]{0:T(128)}, u32[]{:S(2)}, u32[]{:S(2)}) collective-permute-start(f32[16]{0:T(128)} %get-tuple-element.101), channel_id=1, source_target_pairs={{0,8},{8,16},{16,24},{1,9},{9,17},{17,25},{2,10},{10,18},{18,26},{... | collective-permute-start | bytes 200 | tf_op jit(solution)/shard_map/ppermute | solution.py:18
  112.1 11.4 %copy-start.3 = (f32[32]{0:T(128)S(1)}, f32[32]{0:T(128)}, u32[]{:S(2)}) copy-start(f32[32]{0:T(128)} %copy-done.2) | copy-start | bytes 388
where the time goes:
time: 125 us; the launch traced here: 124 us
  blocking collectives  86.1 us (69%)
  other arithmetic  11.8 us (9%)
  local copies, waits for them, and re-layouts  10.9 us (9%)
  starting transfers between devices  6.42 us (5%)
  matrix products  6.11 us (5%)
  between operations  2.75 us (2%)
    psum x1, blocking collectives, body(): gram, right_side = lax.psum((gram_local, side_local), ('row', 'col'))  42.1 us
    psum x1, blocking collectives, body(): image_own = lax.psum(partial_value, 'col')  25.9 us
    unnamed x2, blocking collectives  18.1 us
    ppermute x1, starting transfers between devices, with_halo(): before = lax.ppermute(last, axis, up)  5.14 us
    concatenate x4, other arithmetic, with_halo(): x = jnp.concatenate([before, x, after], axis=dim)  4.81 us
    another operation x1, local copies, waits for them, and re-layouts, window_cones(): slack_win = jnp.stack([slack_ext[RIM + s:RIM + s + length] for s in shifts])  4.14 us
  transfers between devices with their start and end apart: 2, of which 0 were waited for; matrix products, arithmetic and copies ran while one was open for 5% of the time, Pallas kernels for 0%

commit v1 on v0

--- a/solution.py
+++ b/solution.py
@@ -71,7 +71,8 @@
     partial_value = jnp.zeros((row_block,), jnp.float32) + jnp.dot(
         columns, lax.all_gather(blended, "row", axis=0, tiled=True), precision=HIGH
     )
-    image_own = lax.psum(partial_value, "col")
+    floor_meet = lambda q_in, dev_axis: jax.lax.all_gather(q_in, dev_axis).sum(axis=0)
+    image_own = floor_meet(partial_value, "col")
     head_all = jnp.concatenate(
         [jnp.ones((1,), jnp.float32), (cone_id[1:] != cone_id[:-1]).astype(jnp.float32)]
     )

time: 125 us -> 113 us (0.904)
  blocking collectives: 86.1 us -> 74.1 us
    psum x1 -> x0, blocking collectives: 25.9 us -> none  [body(): image_own = lax.psum(partial_value, 'col')]
    all_gather x0 -> x1, blocking collectives: none -> 14 us  [body(): jax.lax.all_gather(q_in, dev_axis).sum(axis=0)]
where the time goes in v1:
time: 113 us; the launch traced here: 112 us
  blocking collectives  74.1 us (66%)
  other arithmetic  11.8 us (10%)
  local copies, waits for them, and re-layouts  11.1 us (10%)
  starting transfers between devices  6.42 us (6%)
  matrix products  6.11 us (5%)
  between operations  2.76 us (2%)
    psum x1, blocking collectives, body(): gram, right_side = lax.psum((gram_local, side_local), ('row', 'col'))  42.1 us
    unnamed x2, blocking collectives  18.1 us
    all_gather x1, blocking collectives, body(): jax.lax.all_gather(q_in, dev_axis).sum(axis=0)  14 us
    ppermute x1, starting transfers between devices, with_halo(): before = lax.ppermute(last, axis, up)  5.14 us
    concatenate x4, other arithmetic, with_halo(): x = jnp.concatenate([before, x, after], axis=dim)  4.81 us
    another operation x1, local copies, waits for them, and re-layouts, window_cones(): slack_win = jnp.stack([slack_ext[RIM + s:RIM + s + length] for s in shifts])  4.14 us
  transfers between devices with their start and end apart: 2, of which 0 were waited for; matrix products, arithmetic and copies ran while one was open for 5% of the time, Pallas kernels for 0%

profile of v1, /device:TPU:0, one launch (start us, length us, event | category | flops | bytes accessed | tf_op | source)
XLA Modules:
  0.0 112.4 jit_solution(1452194952120421009)
XLA Ops:
  0.6 0.0 copy-start
  0.6 0.0 copy-start.1
  0.7 1.0 convolution_bitcast_fusion.3
  1.7 1.0 fusion.48
  2.7 42.1 %all-reduce.2 = (f32[10,10]{0,1:T(8,128)S(1)}, f32[10]{0:T(128)S(1)}) all-reduce(f32[10,10]{0,1:T(8,128)S(1)} %fusion.48, f32[10]{0:T(128)S(1)} %convolution_bitcast_fusion.3), channel_id=1, replica_groups=mesh['row'=4,'col'=8] {'row','col'}, use_global_device_ids=true, to_apply=%region_0.0 | all-reduce | flops 110 | bytes 880 | tf_op jit(solution)/shard_map/psum | solution.py:67
  44.7 0.6 select_reduce_fusion.1
  46.0 0.1 copy.20
  46.1 0.9 cholesky.17
  47.0 0.1 copy.21
  47.1 0.1 select_reduce_fusion
  47.2 0.6 compare_reduce_fusion
  47.9 0.6 select_select_fusion
  48.5 0.1 copy.23
  48.6 0.8 custom-call.10
  49.4 0.1 convolution_bitcast_fusion.2
  49.5 0.1 convolution_bitcast_fusion.1
  49.7 1.4 %fusion.56 = (u32[1]{0:T(128)}, u32[1]{0:T(128)}) fusion(u32[32]{0:T(128)} %constant.89, u32[]{:T(128)S(6)} %add.50, u32[]{:T(128)S(6)} %add.47), kind=kLoop, calls=%fused_computation.136 | loop fusion | bytes 24
  51.7 0.9 fusion
  52.6 0.5 copy-done.2
  53.1 0.2 dynamic-update-slice.3
  53.3 9.7 %all-reduce = f32[128]{0:T(128)S(1)} all-reduce(f32[128]{0:T(128)S(1)} %dynamic-update-slice.3), channel_id=1, replica_groups=mesh['row'=4,'col'=8] {'row'}, use_global_device_ids=true, to_apply=%add | all-reduce | flops 128 | bytes 1024
  63.0 1.8 %fusion.43 = f32[1,4096]{1,0:T(1,128)S(1)} fusion(f32[4096,128]{1,0:T(8,128)S(1)} %copy-done, f32[128]{0:T(128)S(1)} %all-reduce), kind=kOutput, calls=%fused_computation.123 | convolution fusion | flops 6291456 | bytes 2114048 | tf_op jit(solution)/shard_map/dot_general | solution.py:71
  64.8 14.0 %all-gather = f32[32768]{0:T(1024)S(1)} all-gather(f32[4096]{0:T(1024)S(1)} %bitcast.210), channel_id=2, replica_groups=mesh['row'=4,'col'=8] {'col'}, dimensions={0}, use_global_device_ids=true | all-gather | bytes 147456 | tf_op jit(solution)/shard_map/all_gather | solution.py:74
  78.9 0.7 dynamic-slice_subtract_fusion
  79.6 0.6 fusion.55
  80.2 1.3 %collective-permute-start.1 = (f32[16]{0:T(128)}, f32[16]{0:T(128)}, u32[]{:S(2)}, u32[]{:S(2)}) collective-permute-start(f32[16]{0:T(128)} %get-tuple-element.100), channel_id=1, source_target_pairs={{8,0},{16,8},{24,16},{9,1},{17,9},{25,17},{10,2},{18,10},{26,18},{... | collective-permute-start | bytes 200 | tf_op jit(solution)/shard_map/ppermute | solution.py:19
  81.5 5.1 %collective-permute-start = (f32[16]{0:T(128)}, f32[16]{0:T(128)}, u32[]{:S(2)}, u32[]{:S(2)}) collective-permute-start(f32[16]{0:T(128)} %get-tuple-element.101), channel_id=1, source_target_pairs={{0,8},{8,16},{16,24},{1,9},{9,17},{17,25},{2,10},{10,18},{18,26},{... | collective-permute-start | bytes 200 | tf_op jit(solution)/shard_map/ppermute | solution.py:18
  86.6 0.1 fusion.2
  86.7 0.1 concatenate.41
  86.8 0.1 concatenate.42
  86.9 0.8 fusion.54
  87.7 0.2 fusion.52
  87.9 0.3 fusion.51
  88.2 0.3 fusion.53
  89.1 0.8 stack.351
  89.8 1.6 %stack.319 = s32[31,4096]{1,0:T(8,128)S(1)} concatenate(s32[1,4096]{1,0:T(1,128)} %bitcast.224, s32[1,4096]{1,0:T(1,128)} %bitcast.223, s32[1,4096]{1,0:T(1,128)} %bitcast.222, s32[1,4096]{1,0:T(1,128)} %bitcast.221, s32[1,4096]{1,0:T(1,128)} %bitcast.220, s32[1,4096]{1,0:T(1,128)} %bitcast.219, s32[1,4096]{1,0:T(1,128)} %bitcast.218, s32[1,4096]{1,0:T(1,128)} %bitcast.217, ...), dimensions={0} | concatenate | bytes 1015808 | tf_op jit(solution)/shard_map/stack | solution.py:34
  91.4 0.0 collective-permute-done.1
  91.4 1.1 pad_maximum_fusion
  92.5 1.0 fusion.3
  93.5 0.0 collective-permute-done
  93.5 1.0 fusion.17
  94.5 1.7 %pad_maximum_fusion.1 = (f32[4096]{0:T(1024)S(1)}, f32[4096]{0:T(1024)}, f32[4096]{0:T(1024)}, f32[4096]{0:T(1024)}, f32[4096]{0:T(1024)}, /*index=5*/f32[4096]{...) fusion(f32[4096]{0:T(1024)S(1)} %dynamic-slice_subtract_fusion, f32[16]{0:T(128)} %collective-permute-done), kind=kLoop, calls=%fused_computation.102 | loop fusion | flops 36864 | bytes 163904 | tf_op jit(solution)/shard_map/concatenate | solution.py:20
  96.3 4.1 %stack.383 = f32[31,4096]{1,0:T(8,128)} concatenate(f32[1,4096]{1,0:T(1,128)} %bitcast.202, f32[1,4096]{1,0:T(1,128)} %bitcast.203, f32[1,4096]{1,0:T(1,128)} %bitcast.204, f32[1,4096]{1,0:T(1,128)} %bitcast.205, f32[1,4096]{1,0:T(1,128)} %bitcast.206, f32[1,4096]{1,0:T(1,128)} %bitcast.207, f32[1,4096]{1,0:T(1,128)} %bitcast.208, f32[1,4096]{1,0:T(1,128)} %bitcast.209, ...), dimensions={0} | concatenate | bytes 1015808 | tf_op jit(solution)/shard_map/stack | solution.py:33
  100.4 1.3 %fusion.1 = (f32[4096]{0:T(1024)S(1)}, f32[4096]{0:T(1024)S(1)}) fusion(f32[31,4096]{1,0:T(8,128)} %stack.383, f32[31,4096]{1,0:T(8,128)S(1)} %stack.351, s32[31,4096]{1,0:T(8,128)S(1)} %stack.319, s32[4096]{0:T(1024)S(1)} %get-tuple-element.54), kind=kLoop, calls=%fused_computation.7 | loop fusion | flops 1134592 | bytes 1572864 | tf_op jit(solution)/shard_map/reduce_sum | solution.py:41
  101.7 0.6 fusion.49
  102.3 1.1 convolution_bitcast_fusion.4
  103.4 8.4 %all-reduce.1 = f32[128]{0:T(128)S(1)} all-reduce(f32[128]{0:T(128)S(1)} %convolution_bitcast_fusion.4), channel_id=3, replica_groups=mesh['row'=4,'col'=8] {'row'}, use_global_device_ids=true, to_apply=%region_8.9.clone | all-reduce | flops 128 | bytes 1024
  111.8 0.6 fusion.42
  (12 shorter events, 0.1 us)
Async XLA Ops:
  0.6 62.4 %copy-start = (f32[4096,128]{1,0:T(8,128)S(1)}, f32[4096,128]{1,0:T(8,128)}, u32[]{:S(2)}) copy-start(f32[4096,128]{1,0:T(8,128)} %param.7) | copy-start | bytes 6291460
  0.6 86.0 %copy-start.1 = (s32[16384]{0:T(1024)S(1)}, s32[16384]{0:T(1024)}, u32[]{:S(2)}) copy-start(s32[16384]{0:T(1024)} %param.9) | copy-start | bytes 196612
  52.6 0.5 copy-start.2
  80.2 11.2 %collective-permute-start.1 = (f32[16]{0:T(128)}, f32[16]{0:T(128)}, u32[]{:S(2)}, u32[]{:S(2)}) collective-permute-start(f32[16]{0:T(128)} %get-tuple-element.100), channel_id=1, source_target_pairs={{8,0},{16,8},{24,16},{9,1},{17,9},{25,17},{10,2},{18,10},{26,18},{... | collective-permute-start | bytes 200 | tf_op jit(solution)/shard_map/ppermute | solution.py:19
  81.5 12.0 %collective-permute-start = (f32[16]{0:T(128)}, f32[16]{0:T(128)}, u32[]{:S(2)}, u32[]{:S(2)}) collective-permute-start(f32[16]{0:T(128)} %get-tuple-element.101), channel_id=1, source_target_pairs={{0,8},{8,16},{16,24},{1,9},{9,17},{17,25},{2,10},{10,18},{18,26},{... | collective-permute-start | bytes 200 | tf_op jit(solution)/shard_map/ppermute | solution.py:18
  100.4 11.4 %copy-start.3 = (f32[32]{0:T(128)S(1)}, f32[32]{0:T(128)}, u32[]{:S(2)}) copy-start(f32[32]{0:T(128)} %copy-done.2) | copy-start | bytes 388
